TPU v7x, 32 devices: a whole 2x2x4 slice. The times are simulated.
32 devices in a mesh: ocn: 4 (over z), lon: 8 (over y, x, core).
Axes of the slice: x: 2, y: 2, z: 4, core: 2. Of those that a mesh axis runs over, the one named last changes fastest.
Arguments:
- ocean_state: bfloat16 [4, 3072, 128], P(None, ('ocn', 'lon')), may hold values from -6 to 6
- ice_cover: bfloat16 [3072, 128], P(('ocn', 'lon')), may hold values from 0 to 1
- ice_temp: bfloat16 [3072, 128], P(('ocn', 'lon')), may hold values from -6 to 6
- sea_mask: int32 [3072, 128], P(('ocn', 'lon')), may hold values from 0 to 1
- remap_tiles: bfloat16 [32, 160, 128, 128], P(('ocn', 'lon')), may hold values from 0 to 0.015625
- source_tile: int32 [32, 32, 5], P(('ocn', 'lon')), may hold values from 0 to 95
- send_block: int32 [32, 32, 5], P(('ocn', 'lon')), may hold values from -1 to 49, as said below
- recv_block: int32 [32, 32, 5], P(('ocn', 'lon')), may hold values from -1 to 49, as said below
- atm_state: float32 [4, 1600, 128], P(None, ('ocn', 'lon')), may hold values from -6 to 6
Outputs:
- ocean_fluxes: float32 [6, 3072, 128], P(None, ('ocn', 'lon'))
- atm_fluxes: float32 [6, 1600, 128], P(None, ('ocn', 'lon'))
Inputs may be any that keep to these rules, and one draw needn't show every extreme that they name: `send_block`: -1 marks an empty slot; every slot from a device to itself is filled. recv_block[e, s, c] equals send_block[s, e, c].
All inputs are finite; a program needn't handle non-finite values.
Results may differ from a plain program's by a relative error of at most 0.0019.
Values may be sent and summed in bfloat16 or wider, within the bound.
A program may use at most 64 MiB of HBM per device.

v0:
```python
import jax
import jax.numpy as jnp
from jax import lax
from jax.sharding import PartitionSpec as P

highest = lax.Precision.HIGHEST


def stack_fields(ocean_state, ice_cover, ice_temp, sea_mask):
    sea_frac = sea_mask.astype(jnp.bfloat16)
    fields = jnp.concatenate([ocean_state, ice_cover[None], ice_temp[None]], 0)
    return jnp.concatenate([fields * sea_frac[None], sea_frac[None]], 0)


def bulk_fluxes(gathered, atm_state):
    inverse = 1.0 / jnp.maximum(gathered[6], 0.1)
    surface_temp = gathered[0] * inverse
    current_u = gathered[1] * inverse
    current_v = gathered[2] * inverse
    salinity = gathered[3] * inverse
    ice_frac = gathered[4] * inverse
    ice_surface = gathered[5] * inverse
    slip_east = atm_state[0] - current_u
    slip_north = atm_state[1] - current_v
    wind_speed = jnp.sqrt(slip_east * slip_east + slip_north * slip_north + 0.25)
    open_water = 1.0 - ice_frac
    saturation = 0.5 * jnp.exp(0.2 * surface_temp) * (1.0 - 0.05 * salinity)
    evaporation = 0.3 * open_water * wind_speed * (saturation - atm_state[3])
    heat = (
        0.3
        * wind_speed
        * (open_water * (surface_temp - atm_state[2]) + ice_frac * (ice_surface - atm_state[2]))
        + 2.5 * evaporation
    )
    return jnp.stack(
        [
            0.5 * open_water * wind_speed * slip_east,
            0.5 * open_water * wind_speed * slip_north,
            0.8 * ice_frac * wind_speed * slip_east,
            0.8 * ice_frac * wind_speed * slip_north,
            heat,
            evaporation,
        ],
        0,
    )


def shards(
    ocean_state,
    ice_cover,
    ice_temp,
    sea_mask,
    remap_tiles,
    source_tile,
    send_block,
    recv_block,
    atm_state,
):
    rows_ocn = lax.axis_size("ocn")
    rows_lon = lax.axis_size("lon")
    peers = rows_ocn * rows_lon
    slots = remap_tiles.shape[1]
    capacity = slots // peers
    width = sea_mask.shape[1]
    ocean_tiles = sea_mask.shape[0]
    atm_tiles = atm_state.shape[1]
    tiles = remap_tiles[0]
    sources = source_tile[0].reshape(slots)
    targets = send_block[0].reshape(slots)
    filled = (targets >= 0).astype(jnp.float32)
    stacked = stack_fields(ocean_state, ice_cover, ice_temp, sea_mask)
    picked = jnp.take(stacked, sources, axis=1)
    contrib = jnp.einsum("fsi,sij->sfj", picked, tiles, preferred_element_type=jnp.float32)
    contrib = (contrib * filled[:, None, None]).astype(jnp.bfloat16)
    arriving = lax.all_to_all(
        contrib.reshape(peers, capacity, 7, width),
        ("ocn", "lon"),
        split_axis=0,
        concat_axis=0,
        tiled=True,
    )
    arriving = arriving.reshape(slots, 7, width)
    blocks = recv_block[0].reshape(slots)
    onehot = (blocks[None, :] == jnp.arange(atm_tiles, dtype=jnp.int32)[:, None]).astype(
        jnp.float32
    )
    gathered = jnp.einsum("bs,sfj->fbj", onehot, arriving.astype(jnp.float32), precision=highest)
    fluxes = bulk_fluxes(gathered, atm_state)
    back = jnp.einsum("bs,fbj->sfj", onehot, fluxes, precision=highest).astype(jnp.bfloat16)
    returning = lax.all_to_all(
        back.reshape(peers, capacity, 6, width),
        ("ocn", "lon"),
        split_axis=0,
        concat_axis=0,
        tiled=True,
    )
    returning = returning.reshape(slots, 6, width)
    owners = (sources[None, :] == jnp.arange(ocean_tiles, dtype=jnp.int32)[:, None]).astype(
        jnp.float32
    ) * filled[None, :]
    terms = jnp.einsum("sfj,sij->sfi", returning, tiles, preferred_element_type=jnp.float32)
    ones_column = jnp.ones((width,), jnp.bfloat16)
    coverage = jnp.einsum("sij,j->si", tiles, ones_column, preferred_element_type=jnp.float32)
    summed = jnp.einsum("bs,sfi->fbi", owners, terms, precision=highest)
    cover = jnp.dot(owners, coverage, precision=highest)
    ocean_fluxes = summed / jnp.maximum(cover, 0.1)[None] * sea_mask.astype(jnp.float32)[None]
    return (ocean_fluxes, fluxes)


def solution(mesh):
    in_specs = (
        P(None, ("ocn", "lon"), None),
        P(("ocn", "lon"), None),
        P(("ocn", "lon"), None),
        P(("ocn", "lon"), None),
        P(("ocn", "lon"), None, None, None),
        P(("ocn", "lon"), None, None),
        P(("ocn", "lon"), None, None),
        P(("ocn", "lon"), None, None),
        P(None, ("ocn", "lon"), None),
    )
    out_specs = (P(None, ("ocn", "lon"), None), P(None, ("ocn", "lon"), None))
    return jax.shard_map(shards, mesh=mesh, in_specs=in_specs, out_specs=out_specs, check_vma=False)
```

profile of v0, /device:TPU:0, one launch (start us, length us, event | category | flops | bytes accessed | tf_op | source)
XLA Modules:
  0.0 53.4 jit_solution(2942145003198176531)
XLA Ops:
  0.6 0.0 copy-start.2
  0.6 0.0 copy-start.1
  0.7 0.8 %copy.29 = s32[1,32,5]{2,1,0:T(8,128)S(1)} copy(s32[1,32,5]{1,0,2:T(1,128)} %param.14) | data formatting | bytes 1280 | tf_op args[5]
  1.4 0.1 reshape_squeeze.7
  1.6 0.1 reshape_squeeze.6
  1.7 0.9 %fusion.55 = (f32[96,128]{1,0:T(8,128)S(1)}, bf16[96,128]{1,0:T(8,128)(2,1)S(1)}) fusion(s32[96,128]{1,0:T(8,128)} %param.12), kind=kLoop, calls=%fused_computation.76 | loop fusion | flops 24576 | bytes 122880 | tf_op jit(solution)/shard_map/convert_element_type | solution.py:106
  2.6 0.9 %copy.30 = bf16[4,96,128]{2,0,1:T(4,128)(2,1)S(1)} copy(bf16[4,96,128]{2,1,0:T(8,128)(2,1)} %param.9) | data formatting | bytes 196608 | tf_op args[0]
  3.5 0.8 %copy.31 = bf16[1,96,128]{2,0,1:T(2,128)(2,1)S(1)} copy(bf16[1,96,128]{2,1,0:T(8,128)(2,1)} %bitcast.46) | data formatting | bytes 49152 | tf_op jit(solution)/shard_map/broadcast_in_dim | solution.py:11
  4.3 0.8 %copy.32 = bf16[1,96,128]{2,0,1:T(2,128)(2,1)S(1)} copy(bf16[1,96,128]{2,1,0:T(8,128)(2,1)} %bitcast.47) | data formatting | bytes 49152 | tf_op jit(solution)/shard_map/broadcast_in_dim | solution.py:11
  5.2 0.7 %compare_convert_fusion = f32[1,32,5]{1,0,2:T(1,128)S(1)} fusion(s32[1,32,5]{1,0,2:T(1,128)} %param.15), kind=kLoop, calls=%fused_computation.65 | loop fusion | flops 320 | bytes 1280 | tf_op jit(solution)/shard_map/convert_element_type | solution.py:70
  5.8 0.1 copy.35
  5.9 0.1 reshape.75
  6.0 0.2 maximum_multiply_fusion
  6.2 0.1 pad_maximum_fusion
  6.4 0.7 %gather_fusion = bf16[160,7,128]{2,1,0:T(8,128)(2,1)S(1)} fusion(bf16[7,96,128]{2,0,1:T(8,128)(2,1)S(1)} %pad_maximum_fusion, s32[1024]{0:T(1024)S(1)} %pad_clamp_fusion), kind=kCustom, calls=%fused_computation | custom fusion | bytes 574080 | tf_op jit(solution)/shard_map/jit(_take)/gather | solution.py:72
  7.1 4.7 %fusion.9 = bf16[160,7,128]{2,1,0:T(8,128)(2,1)} fusion(bf16[1,160,128,128]{3,2,1,0:T(8,128)(2,1)} %param.13, bf16[160,7,128]{2,1,0:T(8,128)(2,1)S(1)} %gather_fusion, f32[160]{0:T(256)S(1)} %reshape.75, pred[160]{0:T(512)(128)(4,1)S(1)} %compare_and_fusion), kind=kOutput, calls=%fused_computation.8 | convolution fusion | flops 37130240 | bytes 5817120 | tf_op jit(solution)/shard_map/fsi,sij->sfj/dot_general | solution.py:73
  11.8 7.3 %all-to-all-start = ((bf16[32,5,7,128]{3,2,1,0:T(8,128)(2,1)}), bf16[32,5,7,128]{3,2,1,0:T(8,128)(2,1)S(1)}, u32[]{:S(2)}, u32[]{:S(2)}) async-start(bf16[32,5,7,128]{3,2,1,0:T(8,128)(2,1)} %bitcast.7), calls=%async_computation | async-start | bytes 655360 | tf_op jit(solution)/shard_map/all_to_all | solution.py:75
  19.1 0.0 copy-done.2
  19.2 0.1 copy.28
  19.2 0.1 eq.28
  19.3 0.0 copy-done.1
  19.4 0.1 fusion.54
  19.4 11.7 %all-to-all-done = bf16[32,5,7,128]{3,2,1,0:T(8,128)(2,1)S(1)} async-done(((bf16[32,5,7,128]{3,2,1,0:T(8,128)(2,1)}), bf16[32,5,7,128]{3,2,1,0:T(8,128)(2,1)S(1)}, u32[]{:S(2)}, u32[]{:S(2)}) %all-to-all-start) | async-done | bytes 286752 | tf_op jit(solution)/shard_map/all_to_all | solution.py:75
  31.2 0.2 convolution_bitcast_fusion.1
  31.6 0.0 copy-start
  31.6 0.4 convolution_convert_fusion
  32.0 0.8 %copy.41 = bf16[160,6,128]{2,1,0:T(8,128)(2,1)} copy(bf16[160,6,128]{2,0,1:T(8,128)(2,1)S(1)} %convolution_convert_fusion) | data formatting | bytes 491520 | tf_op jit(solution)/shard_map/convert_element_type | solution.py:89
  32.8 2.6 %all-to-all-start.1 = ((bf16[32,5,6,128]{3,2,1,0:T(8,128)(2,1)}), bf16[32,5,6,128]{3,2,1,0:T(8,128)(2,1)S(1)}, u32[]{:S(2)}, u32[]{:S(2)}) async-start(bf16[32,5,6,128]{3,2,1,0:T(8,128)(2,1)} %bitcast.10), calls=%async_computation.1 | async-start | bytes 655360 | tf_op jit(solution)/shard_map/all_to_all | solution.py:90
  35.4 3.9 %fusion = f32[1,160,128]{2,0,1:T(1,128)S(1)} fusion(bf16[1,160,128,128]{3,2,1,0:T(8,128)(2,1)} %param.13), kind=kOutput, calls=%fused_computation.1 | convolution fusion | flops 5242880 | bytes 5324800 | tf_op jit(solution)/shard_map/sij,j->si/dot_general | solution.py:103
  39.4 0.5 convolution_maximum_fusion
  39.9 7.6 %all-to-all-done.1 = bf16[32,5,6,128]{3,2,1,0:T(8,128)(2,1)S(1)} async-done(((bf16[32,5,6,128]{3,2,1,0:T(8,128)(2,1)}), bf16[32,5,6,128]{3,2,1,0:T(8,128)(2,1)S(1)}, u32[]{:S(2)}, u32[]{:S(2)}) %all-to-all-start.1) | async-done | bytes 245792 | tf_op jit(solution)/shard_map/all_to_all | solution.py:90
  47.5 4.6 %fusion.2 = f32[160,6,128]{2,1,0:T(8,128)S(1)} fusion(bf16[160,6,128]{2,1,0:T(8,128)(2,1)S(1)} %bitcast.42, bf16[1,160,128,128]{3,2,1,0:T(8,128)(2,1)} %param.13), kind=kOutput, calls=%fused_computation.3 | convolution fusion | flops 31457280 | bytes 5980160 | tf_op jit(solution)/shard_map/sfj,sij->sfi/dot_general | solution.py:101
  52.1 0.0 copy-done
  52.1 1.3 %fusion.13 = f32[6,96,128]{2,1,0:T(8,128)} fusion(f32[160,6,128]{2,1,0:T(8,128)S(1)} %fusion.2, f32[96,128]{1,0:T(8,128)S(1)} %get-tuple-element.10, f32[96,128]{1,0:T(8,128)S(1)} %convolution_maximum_fusion, f32[160]{0:T(256)S(1)} %reshape.75, s32[160]{0:T(256)S(1)} %reshape_squeeze.6), kind=kOutput, calls=%fused_computation.12 | convolution fusion | flops 141735936 | bytes 886016 | tf_op jit(solution)/shard_map/bs,sfi->fbi/dot_general | solution.py:104
  (10 shorter events, 0.3 us)
Async XLA Ops:
  0.6 18.5 %copy-start.2 = (s32[1,32,5]{1,0,2:T(1,128)S(1)}, s32[1,32,5]{1,0,2:T(1,128)}, u32[]{:S(2)}) copy-start(s32[1,32,5]{1,0,2:T(1,128)} %param.16) | copy-start | bytes 1924
  0.6 18.7 %copy-start.1 = (f32[4,50,128]{2,0,1:T(4,128)S(1)}, f32[4,50,128]{2,0,1:T(4,128)}, u32[]{:S(2)}) copy-start(f32[4,50,128]{2,0,1:T(4,128)} %param.17) | copy-start | bytes 307204
  11.8 19.4 %all-to-all-start = ((bf16[32,5,7,128]{3,2,1,0:T(8,128)(2,1)}), bf16[32,5,7,128]{3,2,1,0:T(8,128)(2,1)S(1)}, u32[]{:S(2)}, u32[]{:S(2)}) async-start(bf16[32,5,7,128]{3,2,1,0:T(8,128)(2,1)} %bitcast.7), calls=%async_computation | async-start | bytes 655360 | tf_op jit(solution)/shard_map/all_to_all | solution.py:75
  31.6 20.5 %copy-start = (f32[6,50,128]{2,1,0:T(8,128)}, f32[6,50,128]{2,1,0:T(8,128)S(1)}, u32[]{:S(2)}) copy-start(f32[6,50,128]{2,1,0:T(8,128)S(1)} %fusion.46) | copy-start | bytes 460804
  32.8 14.6 %all-to-all-start.1 = ((bf16[32,5,6,128]{3,2,1,0:T(8,128)(2,1)}), bf16[32,5,6,128]{3,2,1,0:T(8,128)(2,1)S(1)}, u32[]{:S(2)}, u32[]{:S(2)}) async-start(bf16[32,5,6,128]{3,2,1,0:T(8,128)(2,1)} %bitcast.10), calls=%async_computation.1 | async-start | bytes 655360 | tf_op jit(solution)/shard_map/all_to_all | solution.py:90
where the time goes:
time: 54 us; the launch traced here: 53.4 us
  waiting for transfers between devices  19.4 us (36%)
  matrix products  15.7 us (29%)
  starting transfers between devices  9.91 us (18%)
  local copies, waits for them, and re-layouts  5.56 us (10%)
  other arithmetic  2.1 us (4%)
  between operations  0.82 us (2%)
    all_to_all x1, waiting for transfers between devices, shards(): lax.all_to_all(contrib.reshape(peers, capacity, 7, width), ('ocn', 'lon')...  11.7 us
    all_to_all x1, waiting for transfers between devices, shards(): lax.all_to_all(back.reshape(peers, capacity, 6, width), ('ocn', 'lon'), s...  7.62 us
    all_to_all x1, starting transfers between devices, shards(): lax.all_to_all(contrib.reshape(peers, capacity, 7, width), ('ocn', 'lon')...  7.33 us
    dot_general x1, matrix products, shards(): jnp.einsum('fsi,sij->sfj', picked, tiles, preferred_element_type=jnp.floa...  4.73 us
    dot_general x1, matrix products, shards(): jnp.einsum('sfj,sij->sfi', returning, tiles, preferred_element_type=jnp.f...  4.63 us
    dot_general x1, matrix products, shards(): jnp.einsum('sij,j->si', tiles, ones_column, preferred_element_type=jnp.fl...  3.93 us
    all_to_all x1, starting transfers between devices, shards(): lax.all_to_all(back.reshape(peers, capacity, 6, width), ('ocn', 'lon'), s...  2.59 us
    unnamed x9, local copies, waits for them, and re-layouts  1.85 us
  transfers between devices with their start and end apart: 2, of which 2 were waited for; matrix products, arithmetic and copies ran while one was open for 9% of the time, Pallas kernels for 0%

commit v1 on v0

v1 whole, which is shorter than its diff:
```python
import functools

import jax
import jax.numpy as jnp
from jax import lax
from jax.experimental import pallas as pl
from jax.experimental.pallas import tpu as pltpu
from jax.sharding import PartitionSpec as P

MESH = pl.DeviceIdType.MESH
F32 = jnp.float32
BF16 = jnp.bfloat16
ROWS = 8


def round_up(value, step):
    return (value + step - 1) // step * step


def fluxes_of(gathered, wind_u, wind_v, air_temp, humidity):
    inverse = 1.0 / jnp.maximum(gathered[6], 0.1)
    surface_temp, current_u, current_v, salinity, ice_frac, ice_surface = (
        gathered[f] * inverse for f in range(6)
    )
    slip_east = wind_u - current_u
    slip_north = wind_v - current_v
    speed = jnp.sqrt(slip_east * slip_east + slip_north * slip_north + 0.25)
    open_water = 1.0 - ice_frac
    saturation = 0.5 * jnp.exp(0.2 * surface_temp) * (1.0 - 0.05 * salinity)
    evaporation = 0.3 * open_water * speed * (saturation - humidity)
    heat = (
        0.3
        * speed
        * (open_water * (surface_temp - air_temp) + ice_frac * (ice_surface - air_temp))
        + 2.5 * evaporation
    )
    return (
        0.5 * open_water * speed * slip_east,
        0.5 * open_water * speed * slip_north,
        0.8 * ice_frac * speed * slip_east,
        0.8 * ice_frac * speed * slip_north,
        heat,
        evaporation,
    )


def kernel(
    n_lon, n, cap, ocean_tiles, atm_tiles, unroll,
    state_hbm, cover_hbm, temp_hbm, mask_hbm, tiles_hbm, source_hbm, recv_hbm, atm_hbm,
    ocean_out, atm_out,
    state, ice_cover, ice_temp, mask, tiles, source_v, recv_v, atm,
    picked, arrived, send_one, recv_one, send_two, recv_two,
    in_sems, tile_sems, sent_one, got_one, sent_two, got_two,
):
    atm_rows = round_up(atm_tiles, 8)
    block = cap * ROWS
    groups = n // unroll
    me = lax.axis_index("ocn") * n_lon + lax.axis_index("lon")

    def place(device):
        return (device // n_lon, device % n_lon)

    def peer_of(i):
        away = (i + 1) // 2
        return (me + n // 2 + jnp.where(i % 2 == 0, away, n - away)) % n

    barrier = pltpu.get_barrier_semaphore()

    def greet(i, carry):
        pl.semaphore_signal(
            barrier, inc=1, device_id=place((me + i) % n), device_id_type=MESH
        )
        return carry

    lax.fori_loop(1, n, greet, 0)

    loads = [
        pltpu.make_async_copy(src, dst, in_sems.at[k])
        for k, (src, dst) in enumerate(
            (
                (source_hbm, source_v),
                (mask_hbm, mask),
                (state_hbm, state),
                (cover_hbm, ice_cover),
                (temp_hbm, ice_temp),
                (recv_hbm, recv_v),
                (atm_hbm, atm.at[pl.ds(0, 4 * atm_tiles)]),
            )
        )
    ]
    for load in loads:
        load.start()

    def tile_copy(peer):
        return pltpu.make_async_copy(
            tiles_hbm.at[0, pl.ds(peer * cap, cap)],
            tiles.at[pl.ds(peer * cap, cap)],
            tile_sems.at[peer],
        )

    def fetch(i, carry):
        tile_copy(peer_of(i)).start()
        return carry

    lax.fori_loop(0, n, fetch, 0)

    for c in range(cap):
        picked[pl.ds(c * ROWS + 7, n, stride=block), :] = jnp.zeros(
            (n, picked.shape[1]), F32
        )
    for load in loads[:5]:
        load.wait()
    def pick(target, onehot, fields):
        chosen = onehot.T.astype(BF16)
        for f, field in enumerate(fields):
            rows = jnp.dot(chosen, field.astype(BF16), preferred_element_type=F32)
            for c in range(cap):
                target[pl.ds(c * ROWS + f, n, stride=block), :] = rows[
                    c * n : (c + 1) * n
                ]

    sea = mask[...].astype(F32)
    sources = jnp.concatenate([source_v[c] for c in range(cap)], 1)
    owners = (
        lax.broadcasted_iota(jnp.int32, (ocean_tiles, n * cap), 0) == sources
    ).astype(F32)
    fields = [state[f].astype(F32) * sea for f in range(4)]
    fields += [ice_cover[...].astype(F32) * sea, ice_temp[...].astype(F32) * sea, sea]
    pick(picked, owners, fields)
    owners = owners.astype(BF16)

    def remap(peer):
        tile_copy(peer).wait()
        rows = picked[pl.ds(pl.multiple_of(peer * block, block), block), :]
        parts = []
        for c in range(cap):
            parts.append(
                jnp.dot(
                    rows[c * ROWS : (c + 1) * ROWS].astype(BF16),
                    tiles[peer * cap + c],
                    preferred_element_type=F32,
                )
            )
        send_one[peer] = jnp.concatenate(parts, 0).astype(BF16)

    def copy_to(peer, outbox, inbox, sent, got):
        return pltpu.make_async_remote_copy(
            src_ref=outbox.at[peer],
            dst_ref=inbox.at[me],
            send_sem=sent.at[peer],
            recv_sem=got.at[me],
            device_id=place(peer),
            device_id_type=MESH,
        )

    def copy_from(peer, outbox, inbox, sent, got):
        return pltpu.make_async_remote_copy(
            src_ref=outbox.at[peer],
            dst_ref=inbox.at[peer],
            send_sem=sent.at[peer],
            recv_sem=got.at[peer],
            device_id=place(peer),
            device_id_type=MESH,
        )

    first = (send_one, recv_one, sent_one, got_one)
    second = (send_two, recv_two, sent_two, got_two)

    for u in range(unroll):
        remap(peer_of(u))
    pl.semaphore_wait(barrier, n - 1)

    def forward(g, carry):
        for u in range(unroll):
            remap(peer_of(g * unroll + u))
        for u in range(unroll):
            copy_to(peer_of((g - 1) * unroll + u), *first).start()
        return carry

    lax.fori_loop(1, groups, forward, 0)
    for u in range(unroll - 1):
        copy_to(peer_of((groups - 1) * unroll + u), *first).start()

    for load in loads[5:]:
        load.wait()
    atm[pl.ds(4 * atm_tiles, 4 * (atm_rows - atm_tiles)), :] = jnp.zeros(
        (4 * (atm_rows - atm_tiles), atm.shape[1]), F32
    )
    blocks = jnp.concatenate([recv_v[c] for c in range(cap)], 1)
    onehot = (
        lax.broadcasted_iota(jnp.int32, (atm_rows, n * cap), 0) == blocks
    ).astype(F32)

    def rows_of(f):
        return jnp.concatenate(
            [arrived[pl.ds(c * ROWS + f, n, stride=block), :] for c in range(cap)], 0
        )

    def keep(peer, inbox):
        arrived[pl.ds(pl.multiple_of(peer * block, block), block), :] = inbox[
            peer
        ].astype(F32)

    keep(me, send_one)

    def receive(i, carry):
        peer = (me + i) % n
        copy_from(peer, *first).wait_recv()
        keep(peer, recv_one)
        return carry

    lax.fori_loop(1, n, receive, 0)
    gathered = [
        jnp.dot(onehot.astype(BF16), rows_of(f).astype(BF16), preferred_element_type=F32)
        for f in range(7)
    ]
    air = [atm[pl.ds(k, atm_rows, stride=4), :] for k in range(4)]
    fluxes = fluxes_of(gathered, *air)
    for f, flux in enumerate(fluxes):
        atm_out[f] = flux[:atm_tiles]
    pick(picked, onehot, fluxes + (jnp.ones_like(fluxes[0]),))

    def answer(peer):
        send_two[peer] = picked[
            pl.ds(pl.multiple_of(peer * block, block), block), :
        ].astype(BF16)

    for u in range(unroll):
        answer(peer_of(u))

    def backward(g, carry):
        for u in range(unroll):
            answer(peer_of(g * unroll + u))
        for u in range(unroll):
            copy_to(peer_of((g - 1) * unroll + u), *second).start()
        return carry

    lax.fori_loop(1, groups, backward, 0)
    for u in range(unroll - 1):
        copy_to(peer_of((groups - 1) * unroll + u), *second).start()

    def spread(peer, inbox):
        back = inbox[peer].astype(F32)
        parts = []
        for c in range(cap):
            parts.append(
                lax.dot_general(
                    back[c * ROWS : (c + 1) * ROWS].astype(BF16),
                    tiles[peer * cap + c],
                    (((1,), (1,)), ((), ())),
                    preferred_element_type=F32,
                )
            )
        arrived[pl.ds(pl.multiple_of(peer * block, block), block), :] = jnp.concatenate(
            parts, 0
        )

    def finish(g, carry):
        peers = [peer_of(n - 1 - g * unroll - u) for u in range(unroll)]
        for peer in peers:
            copy_from(peer, *second).wait_recv()
        for peer in peers:
            spread(peer, recv_two)
        return carry

    spread(me, send_two)
    peers = [peer_of(n - 1 - u) for u in range(1, unroll)]
    for peer in peers:
        copy_from(peer, *second).wait_recv()
    for peer in peers:
        spread(peer, recv_two)
    lax.fori_loop(1, groups, finish, 0)

    def total_of(f):
        rows = rows_of(f)
        high = rows.astype(BF16)
        low = (rows - high.astype(F32)).astype(BF16)
        return jnp.dot(owners, high, preferred_element_type=F32) + jnp.dot(
            owners, low, preferred_element_type=F32
        )

    scale = mask[...].astype(F32) / jnp.maximum(total_of(6), 0.1)
    for f in range(6):
        ocean_out[f] = total_of(f) * scale

    def drain(i, carry):
        peer = (me + i) % n
        copy_to(peer, *first).wait_send()
        copy_to(peer, *second).wait_send()
        return carry

    lax.fori_loop(1, n, drain, 0)


def shards(
    ocean_state,
    ice_cover,
    ice_temp,
    sea_mask,
    remap_tiles,
    source_tile,
    send_block,
    recv_block,
    atm_state,
):
    n_lon = lax.axis_size("lon")
    n = lax.axis_size("ocn") * n_lon
    slots = remap_tiles.shape[1]
    cap = slots // n
    ocean_tiles, width = sea_mask.shape
    atm_tiles = atm_state.shape[1]
    atm_rows = round_up(atm_tiles, 8)
    unroll = 4 if n % 4 == 0 else 1
    sources = source_tile.transpose(2, 0, 1)
    receives = recv_block.transpose(2, 0, 1)
    air = atm_state.transpose(1, 0, 2).reshape(4 * atm_tiles, width)
    anywhere = pl.BlockSpec(memory_space=pl.ANY)
    inside = pl.BlockSpec(memory_space=pltpu.VMEM)
    mail = pltpu.VMEM((n, cap * ROWS, width), BF16)
    sems = pltpu.SemaphoreType.DMA((n,))
    return pl.pallas_call(
        functools.partial(kernel, n_lon, n, cap, ocean_tiles, atm_tiles, unroll),
        out_shape=(
            jax.ShapeDtypeStruct((6, ocean_tiles, width), F32),
            jax.ShapeDtypeStruct((6, atm_tiles, width), F32),
        ),
        in_specs=[anywhere] * 8,
        out_specs=(inside, inside),
        scratch_shapes=[
            pltpu.VMEM(ocean_state.shape, BF16),
            pltpu.VMEM(ice_cover.shape, BF16),
            pltpu.VMEM(ice_temp.shape, BF16),
            pltpu.VMEM(sea_mask.shape, jnp.int32),
            pltpu.VMEM(remap_tiles.shape[1:], BF16),
            pltpu.VMEM(sources.shape, jnp.int32),
            pltpu.VMEM(receives.shape, jnp.int32),
            pltpu.VMEM((4 * atm_rows, width), F32),
            pltpu.VMEM((slots * ROWS, width), F32),
            pltpu.VMEM((slots * ROWS, width), F32),
            mail, mail, mail, mail,
            pltpu.SemaphoreType.DMA((7,)),
            sems, sems, sems, sems, sems,
        ],
        compiler_params=pltpu.CompilerParams(
            collective_id=0, has_side_effects=True, vmem_limit_bytes=60 * 1024 * 1024
        ),
    )(ocean_state, ice_cover, ice_temp, sea_mask, remap_tiles, sources, receives, air)


def solution(mesh):
    one = P(("ocn", "lon"), None)
    field = P(None, ("ocn", "lon"), None)
    slot = P(("ocn", "lon"), None, None)
    return jax.shard_map(
        shards,
        mesh=mesh,
        in_specs=(
            field, one, one, one,
            P(("ocn", "lon"), None, None, None),
            slot, slot, slot, field,
        ),
        out_specs=(field, field),
        check_vma=False,
    )
```

time: 54 us -> 38.3 us (0.71)
  Pallas kernels: 0 us -> 34.2 us
  waiting for transfers between devices: 19.4 us -> 0 us
  matrix products: 15.7 us -> 0 us
  starting transfers between devices: 9.91 us -> 0 us
  local copies, waits for them, and re-layouts: 5.56 us -> 3.29 us
  other arithmetic: 2.1 us -> 0 us
    pallas_call x0 -> x1, Pallas kernels: none -> 34.2 us  [shards(): pl.pallas_call(functools.partial(kernel, n_lon, n, cap, ocean_tiles, atm_...]
    all_to_all x2 -> x0, waiting for transfers between devices: 19.4 us -> none  [the longest x1 11.7 us: shards(): lax.all_to_all(contrib.reshape(peers, capacity, 7, width), ('ocn', 'lon')...]
    dot_general x7 -> x0, matrix products: 15.7 us -> none  [the longest x1 4.73 us: shards(): jnp.einsum('fsi,sij->sfj', picked, tiles, preferred_element_type=jnp.floa...]
    all_to_all x2 -> x0, starting transfers between devices: 9.91 us -> none  [the longest x1 7.33 us: shards(): lax.all_to_all(contrib.reshape(peers, capacity, 7, width), ('ocn', 'lon')...]
    broadcast_in_dim x3 -> x0, local copies, waits for them, and re-layouts: 1.6 us -> none  [the longest x2 1.56 us: stack_fields(): fields = jnp.concatenate([ocean_state, ice_cover[None], ice_temp[None]], 0)]
    convert_element_type x2 -> x0, other arithmetic: 1.58 us -> none  [the longest x1 0.89 us: shards(): sea_mask.astype(jnp.float32)[None]]
    unnamed x9 -> x2, local copies, waits for them, and re-layouts: 1.85 us -> 3.29 us
    convert_element_type x3 -> x0, local copies, waits for them, and re-layouts: 1.02 us -> none  [the longest x1 0.82 us: shards(): jnp.einsum('bs,fbj->sfj', onehot, fluxes, precision=highest)]
  transfers between devices with their start and end apart: 2 -> 0, of which waited for: 2 -> 0; matrix products, arithmetic and copies ran while one was open for 9% -> 0% of each run, Pallas kernels for 0% -> 0%
where the time goes in v1:
time: 38.3 us; the launch traced here: 38.1 us
  Pallas kernels  34.2 us (89%)
  local copies, waits for them, and re-layouts  3.29 us (9%)
  between operations  0.64 us (2%)
    pallas_call x1, Pallas kernels, shards(): pl.pallas_call(functools.partial(kernel, n_lon, n, cap, ocean_tiles, atm_...  34.2 us
    unnamed x2, local copies, waits for them, and re-layouts  3.29 us

profile of v1, /device:TPU:0, one launch (start us, length us, event | category | flops | bytes accessed | tf_op | source)
XLA Modules:
  0.0 38.1 jit_solution(16385913174487965915)
XLA Ops:
  0.6 34.2 %shard_map.95 = (f32[6,96,128]{2,1,0:T(8,128)}, f32[6,50,128]{2,1,0:T(8,128)}) custom-call(bf16[4,96,128]{2,1,0:T(8,128)(2,1)} %state_hbm.1, bf16[96,128]{1,0:T(8,128)(2,1)} %cover_hbm.1, bf16[96,128]{1,0:T(8,128)(2,1)} %temp_hbm.1, s32[96,128]{1,0:T(8,128)} %mask_hbm.1, bf16[1,160,128,128]{3,2,1,0:T(8,128)(2,1)} %tiles_hbm.1, s32[5,1,32]{2,1,0:T(1,128)} %bitcast.6, ...), custom_call_target="tpu_custom_call" | custom-call | tf_op jit(solution)/shard_map/pallas_call | solution.py:321
  34.8 1.7 %copy.12 = f32[6,96,128]{2,1,0:T(8,128)} copy(f32[6,96,128]{2,1,0:T(8,128)} %get-tuple-element.4) | data formatting | bytes 589824
  36.5 1.6 %copy.13 = f32[6,50,128]{2,1,0:T(8,128)} copy(f32[6,50,128]{2,1,0:T(8,128)} %get-tuple-element.5) | data formatting | bytes 307200
